TPU v7x, 32 devices: a whole 2x2x4 slice. The times are simulated.
32 devices in a mesh: sky: 8 (over y, x, core), tm: 4 (over z).
Axes of the slice: x: 2, y: 2, z: 4, core: 2. Of those that a mesh axis runs over, the one named last changes fastest.
Arguments:
- obs_source: int32 [131072], P(('sky', 'tm')), may hold values from 0 to 1023
- obs_knot: int32 [131072], P(('sky', 'tm')), may hold values from 0 to 2047, as said below
- obs_count: int32 [32], P(('sky', 'tm')), may hold values from 256 to 4096, as said below
- src_design: float32 [5, 131072], P(None, ('sky', 'tm')), may hold values from -3 to 3
- att_design: float32 [4, 131072], P(None, ('sky', 'tm')), may hold values from -6 to 6
- obs_phase: float32 [131072], P(('sky', 'tm')), may hold values from 0 to 1
- obs_value: float32 [131072], P(('sky', 'tm')), may hold values from -6 to 6
- src_prior: float32 [5, 8192], P(None, 'sky'), may hold values from 1 to 16
Outputs:
- att_solution: float32 [4, 4, 2048], P(None, 'tm', 'sky')
- att_residual: float32 [4, 4, 2048], P(None, 'tm', 'sky')
- source_solution: float32 [5, 8192], P(None, 'sky')
Inputs may be any that keep to these rules, and one draw needn't show every extreme that they name: Block b holds the 4096 observation slots o with o // 4096 = b; with i = b // 4 its sources are the sources i * 1024 + obs_source. With j = b % 4 for the observation's block b, its four spline knots are j * 2048 + obs_knot and the next three. In every block, each range of 256 values r * 256 to r * 256 + 255 of obs_knot holds exactly 512 of the block's slots. `obs_count`: each count is 4096 divided by 1, 2, 4, 8 or 16; the live slots of a block are its first ones; some block is full.
All inputs are finite; a program needn't handle non-finite values.
Results may differ from a plain program's by a relative error of at most 0.0001.
Values sent between devices are 32-bit elements; how exact they have to be, the bound alone decides.
A program may use at most 64 MiB of HBM per device.

v0:
```python
import jax
import jax.numpy as jnp
from jax import lax
from jax.sharding import PartitionSpec as P

ITERS = 2
SRC_DEV = 1024
KN_DEV = 256


damping = 0.5
entry_pairs = [(row_at, col_at) for row_at in range(5) for col_at in range(row_at + 1)]


def shifted(value, axis, steps):
    count = lax.axis_size(axis)
    first, last = (max(0, -steps), min(count, count - steps))
    return lax.ppermute(value, axis, [(source, source + steps) for source in range(first, last)])


def spline_taps(phase):
    squared = phase * phase
    cubed = squared * phase
    rest = 1.0 - phase
    return (
        rest * rest * rest / 6.0,
        (3.0 * cubed - 6.0 * squared + 4.0) / 6.0,
        (-3.0 * cubed + 3.0 * squared + 3.0 * phase + 1.0) / 6.0,
        cubed / 6.0,
    )


def factorize(normal):
    factor = {}
    for row_at in range(5):
        for col_at in range(row_at + 1):
            running = normal[row_at, col_at]
            for inner_at in range(col_at):
                running = running - factor[row_at, inner_at] * factor[col_at, inner_at]
            if row_at == col_at:
                factor[row_at, row_at] = jnp.sqrt(running)
            else:
                factor[row_at, col_at] = running / factor[col_at, col_at]
    return factor


def chol_solve(factor, target):
    forward = []
    for row_at in range(5):
        running = target[row_at]
        for inner_at in range(row_at):
            running = running - factor[row_at, inner_at] * forward[inner_at]
        forward.append(running / factor[row_at, row_at])
    result = [None] * 5
    for row_at in reversed(range(5)):
        running = forward[row_at]
        for inner_at in range(row_at + 1, 5):
            running = running - factor[inner_at, row_at] * result[inner_at]
        result[row_at] = running / factor[row_at, row_at]
    return jnp.stack(result)


def source_total(source, rows, count):
    return jnp.zeros((rows.shape[0], count), jnp.float32).at[:, source].add(rows)


def knot_values(padded, knot, design, tap_weights):
    summed = jnp.zeros(knot.shape, jnp.float32)
    for tap_at in range(4):
        picked = jnp.take(padded, knot + tap_at, axis=1)
        summed = summed + tap_weights[tap_at] * jnp.sum(design * picked, axis=0)
    return summed


def knot_total(knot, design, tap_weights, weight_vec, extent):
    summed = jnp.zeros((design.shape[0], extent + 3), jnp.float32)
    for tap_at in range(4):
        summed = summed.at[:, knot + tap_at].add(design * (tap_weights[tap_at] * weight_vec))
    return summed


def eliminate(factor, source, design, values_obs, source_sums):
    solved = chol_solve(factor, [source_sums[row_at] for row_at in range(5)])
    fitted = jnp.sum(design * jnp.take(solved, source, axis=1), axis=0)
    return values_obs - fitted


def shards(
    obs_source, obs_knot, obs_count, src_design, att_design, obs_phase, obs_value, src_prior
):
    sky_count = lax.axis_size("sky")
    seg_knots = KN_DEV * sky_count
    slot_count = obs_source.shape[0]
    live_mask = (jnp.arange(slot_count, dtype=jnp.int32) < obs_count[0]).astype(jnp.float32)
    src_rows = src_design * live_mask
    att_rows = att_design * live_mask
    observed = obs_value * live_mask
    tap_weights = spline_taps(obs_phase)
    products = jnp.stack(
        [src_rows[row_at] * src_rows[col_at] for row_at, col_at in entry_pairs]
        + [src_rows[row_at] * observed for row_at in range(5)]
    )
    sums = lax.psum(source_total(obs_source, products, SRC_DEV), "tm")
    normal = {}
    for entry_at, pair in enumerate(entry_pairs):
        normal[pair] = sums[entry_at] + (src_prior[pair[0]] if pair[0] == pair[1] else 0.0)
    factor = factorize(normal)

    def source_part(values_obs):
        return lax.psum(source_total(obs_source, src_rows * values_obs, SRC_DEV), "tm")

    def along_knots(field):
        segment = lax.all_gather(field, "sky", axis=1, tiled=True)
        next_edge = shifted(segment[:, :3], "tm", -1)
        padded = jnp.concatenate([segment, next_edge], axis=1)
        return knot_values(padded, obs_knot, att_rows, tap_weights)

    def back_to_knots(cleaned):
        summed = knot_total(obs_knot, att_rows, tap_weights, cleaned, seg_knots)
        overflow = shifted(summed[:, seg_knots:], "tm", 1)
        partial_value = summed[:, :seg_knots].at[:, :3].add(overflow)
        return lax.psum_scatter(partial_value, "sky", scatter_dimension=1, tiled=True)

    def norm_sum(partial_value):
        return lax.psum(partial_value, ("sky", "tm"))

    cleaned = eliminate(factor, obs_source, src_rows, observed, sums[15:])
    residual = back_to_knots(cleaned)
    solution = jnp.zeros_like(residual)
    direction = residual
    norm_now = norm_sum(jnp.sum(residual * residual))
    for repeat in range(ITERS):
        image_obs = along_knots(direction)
        cleaned = eliminate(factor, obs_source, src_rows, image_obs, source_part(image_obs))
        mapped = back_to_knots(cleaned) + damping * direction
        alpha_step = norm_now / lax.psum(jnp.sum(direction * mapped), ("sky", "tm"))
        solution = solution + alpha_step * direction
        residual = residual - alpha_step * mapped
        norm_next = norm_sum(jnp.sum(residual * residual))
        direction = residual + norm_next / norm_now * direction
        norm_now = norm_next
    fitted = observed - along_knots(solution)
    source_solution = chol_solve(factor, [row for row in source_part(fitted)])
    return (solution[:, None, :], residual[:, None, :], source_solution)


def solution(mesh):
    placed = (
        P(("sky", "tm")),
        P(("sky", "tm")),
        P(("sky", "tm")),
        P(None, ("sky", "tm")),
        P(None, ("sky", "tm")),
        P(("sky", "tm")),
        P(("sky", "tm")),
        P(None, "sky"),
    )
    return jax.shard_map(
        shards,
        mesh=mesh,
        in_specs=placed,
        out_specs=(P(None, "tm", "sky"), P(None, "tm", "sky"), P(None, "sky")),
        check_vma=False,
    )
```

profile of v0, /device:TPU:0, one launch (start us, length us, event | category | flops | bytes accessed | tf_op | source)
XLA Modules:
  0.0 1068.7 jit_solution(9590675632088410657)
XLA Ops:
  11.7 22.5 %scatter_custom_fusion = f32[20,1024]{0,1:T(8,128)S(1)} fusion(s32[4096]{0:T(1024)S(1)} %get-tuple-element.173, f32[4096,20]{1,0:T(8,128)S(1)} %copy.271, f32[]{:T(128)} %constant.111.clone.1), kind=kCustom, calls=%fused_computation.113 | custom fusion | flops 81920 | bytes 81924 | tf_op jit(solution)/shard_map/scatter-add | solution.py:64
  37.1 35.3 %all-reduce.3.cloned.1.call-done = f32[20,1024]{1,0:T(8,128)} async-done(((f32[20,1024]{1,0:T(8,128)}), f32[20,1024]{1,0:T(8,128)}) %all-reduce.3.cloned.1.call-update) | async-done | bytes 81936 | tf_op jit(solution)/shard_map/psum | solution.py:103
  92.0 25.3 %scatter_custom_fusion.1 = f32[4,2051]{0,1:T(8,128)S(1)} fusion(s32[4096]{0:T(1024)} %get-tuple-element.168, f32[4096]{0:T(1024)S(1)} %get-tuple-element.159, f32[]{:T(128)} %constant.111.clone.1, f32[4,4096]{0,1:T(8,128)S(1)} %copy.270, f32[4096]{0:T(1024)S(1)} %fusion.83), kind=kCustom, calls=%fused_computation.77 | custom fusion | flops 49152 | bytes 131632 | tf_op jit(solution)/shard_map/scatter-add | solution.py:78
  117.3 25.4 %scatter_custom_fusion.2 = f32[4,2051]{0,1:T(8,128)S(1)} fusion(f32[4,2051]{0,1:T(8,128)S(1)} %scatter_custom_fusion.1, s32[4096]{0:T(1024)} %get-tuple-element.166, f32[4096]{0:T(1024)S(1)} %get-tuple-element.158, f32[4,4096]{0,1:T(8,128)S(1)} %copy.270, f32[4096]{0:T(1024)S(1)} %fusion.83), kind=kCustom, calls=%fused_computation.75 | custom fusion | flops 49152 | bytes 2162736 | tf_op jit(solution)/shard_map/scatter-add | solution.py:78
  142.6 25.4 %scatter_custom_fusion.3 = f32[4,2051]{0,1:T(8,128)S(1)} fusion(f32[4,2051]{0,1:T(8,128)S(1)} %scatter_custom_fusion.2, s32[4096]{0:T(1024)} %get-tuple-element.167, f32[4096]{0:T(1024)S(1)} %get-tuple-element.157, f32[4,4096]{0,1:T(8,128)S(1)} %copy.270, f32[4096]{0:T(1024)S(1)} %fusion.83), kind=kCustom, calls=%fused_computation.73 | custom fusion | flops 49152 | bytes 2162736 | tf_op jit(solution)/shard_map/scatter-add | solution.py:78
  168.1 25.7 %scatter_custom_fusion.4 = f32[4,2051]{0,1:T(8,128)S(1)} fusion(f32[4,2051]{0,1:T(8,128)S(1)} %scatter_custom_fusion.3, s32[4096]{0:T(1024)S(1)} %get-tuple-element.171, f32[4096]{0:T(1024)S(1)} %get-tuple-element.106, f32[4,4096]{0,1:T(8,128)S(1)} %copy.270, f32[4096]{0:T(1024)S(1)} %fusion.83), kind=kCustom, calls=%fused_computation.71 | custom fusion | flops 49152 | bytes 2162736 | tf_op jit(solution)/shard_map/scatter-add | solution.py:78
  201.6 36.5 %reduce-scatter.10.cloned.1.call-done = f32[256,4]{1,0:T(8,128)} async-done(((f32[2048,4]{1,0:T(8,128)}), f32[256,4]{1,0:T(8,128)}) %reduce-scatter.10.cloned.1.call-update) | async-done | bytes 4112
  322.0 22.8 %scatter_custom_fusion.5 = f32[5,1024]{0,1:T(8,128)S(1)} fusion(s32[4096]{0:T(1024)} %copy-done.35, f32[4096,5]{1,0:T(8,128)} %copy.277, f32[]{:T(128)} %constant.111.clone.1), kind=kCustom, calls=%fused_computation.111 | custom fusion | flops 20480 | bytes 20992 | tf_op jit(solution)/shard_map/scatter-add | solution.py:64
  379.9 25.3 %scatter_custom_fusion.6 = f32[4,2051]{0,1:T(8,128)S(1)} fusion(s32[4096]{0:T(1024)} %get-tuple-element.168, f32[4096]{0:T(1024)S(1)} %get-tuple-element.156, f32[]{:T(128)} %constant.111.clone.1, f32[4,4096]{0,1:T(8,128)S(1)} %copy.270, f32[4096]{0:T(1024)S(1)} %fusion.83), kind=kCustom, calls=%fused_computation.61 | custom fusion | flops 49152 | bytes 131632 | tf_op jit(solution)/shard_map/scatter-add | solution.py:78
  405.1 25.6 %scatter_custom_fusion.7 = f32[4,2051]{0,1:T(8,128)S(1)} fusion(f32[4,2051]{0,1:T(8,128)S(1)} %scatter_custom_fusion.6, s32[4096]{0:T(1024)} %get-tuple-element.166, f32[4096]{0:T(1024)S(1)} %get-tuple-element.155, f32[4,4096]{0,1:T(8,128)S(1)} %copy.270, f32[4096]{0:T(1024)S(1)} %fusion.83), kind=kCustom, calls=%fused_computation.59 | custom fusion | flops 49152 | bytes 2162736 | tf_op jit(solution)/shard_map/scatter-add | solution.py:78
  430.7 25.4 %scatter_custom_fusion.8 = f32[4,2051]{0,1:T(8,128)S(1)} fusion(f32[4,2051]{0,1:T(8,128)S(1)} %scatter_custom_fusion.7, s32[4096]{0:T(1024)} %get-tuple-element.167, f32[4096]{0:T(1024)S(1)} %get-tuple-element.154, f32[4,4096]{0,1:T(8,128)S(1)} %copy.270, f32[4096]{0:T(1024)S(1)} %fusion.83), kind=kCustom, calls=%fused_computation.57 | custom fusion | flops 49152 | bytes 2162736 | tf_op jit(solution)/shard_map/scatter-add | solution.py:78
  456.1 25.4 %scatter_custom_fusion.9 = f32[4,2051]{0,1:T(8,128)S(1)} fusion(f32[4,2051]{0,1:T(8,128)S(1)} %scatter_custom_fusion.8, s32[4096]{0:T(1024)} %copy-done.36, f32[4096]{0:T(1024)S(1)} %get-tuple-element.95, f32[4,4096]{0,1:T(8,128)S(1)} %copy.270, f32[4096]{0:T(1024)S(1)} %fusion.83), kind=kCustom, calls=%fused_computation.55 | custom fusion | flops 49152 | bytes 2162736 | tf_op jit(solution)/shard_map/scatter-add | solution.py:78
  487.9 36.2 %reduce-scatter.12.cloned.1.call-done = f32[256,4]{1,0:T(8,128)} async-done(((f32[2048,4]{1,0:T(8,128)}), f32[256,4]{1,0:T(8,128)}) %reduce-scatter.12.cloned.1.call-update) | async-done | bytes 4112
  525.7 39.5 %all-reduce = (f32[]{:T(128)}, f32[]{:T(128)}) all-reduce(f32[]{:T(128)} %get-tuple-element.72, f32[]{:T(128)} %get-tuple-element.71), channel_id=1, replica_groups=mesh['sky'=8,'tm'=4] {'sky','tm'}, use_global_device_ids=true, to_apply=%region_10.12 | all-reduce | flops 2 | bytes 16 | tf_op jit(solution)/shard_map/psum | solution.py:125
  567.0 41.3 %psum.60 = f32[]{:T(128)} all-reduce(f32[]{:T(128)} %multiply_reduce_fusion.1), channel_id=1, replica_groups=mesh['sky'=8,'tm'=4] {'sky','tm'}, use_global_device_ids=true, to_apply=%region_26.29 | all-reduce | flops 1 | bytes 8 | tf_op jit(solution)/shard_map/psum | solution.py:125
  693.4 22.8 %scatter_custom_fusion.10 = f32[5,1024]{0,1:T(8,128)S(1)} fusion(s32[4096]{0:T(1024)} %copy-done.35, f32[4096,5]{1,0:T(8,128)} %copy.286, f32[]{:T(128)} %constant.111.clone.1), kind=kCustom, calls=%fused_computation.109 | custom fusion | flops 20480 | bytes 20992 | tf_op jit(solution)/shard_map/scatter-add | solution.py:64
  750.3 25.3 %scatter_custom_fusion.11 = f32[4,2051]{0,1:T(8,128)S(1)} fusion(s32[4096]{0:T(1024)} %get-tuple-element.168, f32[4096]{0:T(1024)S(1)} %get-tuple-element.153, f32[]{:T(128)} %constant.111.clone.1, f32[4,4096]{0,1:T(8,128)S(1)} %copy.270, f32[4096]{0:T(1024)S(1)} %fusion.83), kind=kCustom, calls=%fused_computation.45 | custom fusion | flops 49152 | bytes 131632 | tf_op jit(solution)/shard_map/scatter-add | solution.py:78
  775.5 25.4 %scatter_custom_fusion.12 = f32[4,2051]{0,1:T(8,128)S(1)} fusion(f32[4,2051]{0,1:T(8,128)S(1)} %scatter_custom_fusion.11, s32[4096]{0:T(1024)} %get-tuple-element.166, f32[4096]{0:T(1024)S(1)} %get-tuple-element.152, f32[4,4096]{0,1:T(8,128)S(1)} %copy.270, f32[4096]{0:T(1024)S(1)} %fusion.83), kind=kCustom, calls=%fused_computation.43 | custom fusion | flops 49152 | bytes 2162736 | tf_op jit(solution)/shard_map/scatter-add | solution.py:78
  800.9 25.4 %scatter_custom_fusion.13 = f32[4,2051]{0,1:T(8,128)S(1)} fusion(f32[4,2051]{0,1:T(8,128)S(1)} %scatter_custom_fusion.12, s32[4096]{0:T(1024)} %get-tuple-element.167, f32[4096]{0:T(1024)S(1)} %get-tuple-element.151, f32[4,4096]{0,1:T(8,128)S(1)} %copy.270, f32[4096]{0:T(1024)S(1)} %fusion.83), kind=kCustom, calls=%fused_computation.41 | custom fusion | flops 49152 | bytes 2162736 | tf_op jit(solution)/shard_map/scatter-add | solution.py:78
  826.3 25.6 %scatter_custom_fusion.14 = f32[4,2051]{0,1:T(8,128)S(1)} fusion(f32[4,2051]{0,1:T(8,128)S(1)} %scatter_custom_fusion.13, s32[4096]{0:T(1024)} %copy-done.36, f32[4096]{0:T(1024)S(1)} %get-tuple-element.84, f32[4,4096]{0,1:T(8,128)S(1)} %copy.270, f32[4096]{0:T(1024)S(1)} %fusion.83), kind=kCustom, calls=%fused_computation.39 | custom fusion | flops 49152 | bytes 2162736 | tf_op jit(solution)/shard_map/scatter-add | solution.py:78
  857.9 36.8 %reduce-scatter.14.cloned.1.call-done = f32[256,4]{1,0:T(8,128)} async-done(((f32[2048,4]{1,0:T(8,128)}), f32[256,4]{1,0:T(8,128)}) %reduce-scatter.14.cloned.1.call-update) | async-done | bytes 4112
  896.3 39.4 %psum.62 = f32[]{:T(128)} all-reduce(f32[]{:T(128)} %multiply_reduce_fusion), channel_id=1, replica_groups=mesh['sky'=8,'tm'=4] {'sky','tm'}, use_global_device_ids=true, to_apply=%region_40.43 | all-reduce | flops 1 | bytes 8 | tf_op jit(solution)/shard_map/psum | solution.py:136
  1020.1 22.6 %scatter_custom_fusion.15 = f32[5,1024]{0,1:T(8,128)S(1)} fusion(s32[4096]{0:T(1024)} %copy-done.35, f32[4096,5]{1,0:T(8,128)S(1)} %copy.295, f32[]{:T(128)} %constant.111.clone.1), kind=kCustom, calls=%fused_computation.107 | custom fusion | flops 20480 | bytes 20992 | tf_op jit(solution)/shard_map/scatter-add | solution.py:64
  1042.9 17.2 %psum.63 = f32[5,1024]{1,0:T(8,128)S(1)} all-reduce(f32[5,1024]{1,0:T(8,128)S(1)} %copy.296), channel_id=1, replica_groups=mesh['sky'=8,'tm'=4] {'tm'}, use_global_device_ids=true, to_apply=%region_46.49 | all-reduce | flops 5120 | bytes 40960 | tf_op jit(solution)/shard_map/psum | solution.py:110
  (201 shorter events, 371.2 us)
Async XLA Ops:
  7.2 65.2 %all-reduce.3.cloned.1.call-start = ((), (), s32[]{:S(2)}) async-start(), calls=%async_computation.3 | async-start | bytes 196608 | tf_op jit(solution)/shard_map/psum | solution.py:103
  35.0 203.1 %reduce-scatter.10.cloned.1.call-start = ((), (), s32[]{:S(2)}) async-start(), calls=%async_computation.4 | async-start | bytes 1179648
  35.7 132.3 %copy-start.36 = (s32[4096]{0:T(1024)}, s32[4096]{0:T(1024)S(1)}, u32[]{:S(2)}) copy-start(s32[4096]{0:T(1024)S(1)} %get-tuple-element.171) | copy-start | bytes 49156
  35.7 344.0 %copy-start.21 = (pred[4096]{0:T(1024)(128)(4,1)}, pred[4096]{0:T(1024)(128)(4,1)S(1)}, u32[]{:S(2)}) copy-start(pred[4096]{0:T(1024)(128)(4,1)S(1)} %compare_and_fusion.4) | copy-start | bytes 12292
  73.6 288.7 %copy-start.3 = (f32[1,1024]{1,0:T(1,128)}, f32[1,1024]{1,0:T(1,128)S(1)}, u32[]{:S(2)}) copy-start(f32[1,1024]{1,0:T(1,128)S(1)} %get-tuple-element.128) | copy-start | bytes 12292
  73.6 288.7 %copy-start.5 = (f32[1,1024]{1,0:T(1,128)}, f32[1,1024]{1,0:T(1,128)S(1)}, u32[]{:S(2)}) copy-start(f32[1,1024]{1,0:T(1,128)S(1)} %get-tuple-element.129) | copy-start | bytes 12292
  73.6 288.7 %copy-start.7 = (f32[1,1024]{1,0:T(1,128)}, f32[1,1024]{1,0:T(1,128)S(1)}, u32[]{:S(2)}) copy-start(f32[1,1024]{1,0:T(1,128)S(1)} %get-tuple-element.130) | copy-start | bytes 12292
  194.9 4.6 collective-permute-start
  201.5 322.6 %reduce-scatter.12.cloned.1.call-start = ((), (), s32[]{:S(2)}) async-start(), calls=%async_computation.5 | async-start | bytes 1179648
  201.6 109.3 %copy-start.13 = (pred[4096]{0:T(1024)(128)(4,1)}, pred[4096]{0:T(1024)(128)(4,1)S(1)}, u32[]{:S(2)}) copy-start(pred[4096]{0:T(1024)(128)(4,1)S(1)} %get-tuple-element.160) | copy-start | bytes 12292
  201.6 109.3 %copy-start.15 = (pred[4096]{0:T(1024)(128)(4,1)}, pred[4096]{0:T(1024)(128)(4,1)S(1)}, u32[]{:S(2)}) copy-start(pred[4096]{0:T(1024)(128)(4,1)S(1)} %get-tuple-element.161) | copy-start | bytes 12292
  201.6 109.3 %copy-start.17 = (pred[4096]{0:T(1024)(128)(4,1)}, pred[4096]{0:T(1024)(128)(4,1)S(1)}, u32[]{:S(2)}) copy-start(pred[4096]{0:T(1024)(128)(4,1)S(1)} %get-tuple-element.162) | copy-start | bytes 12292
  201.6 109.3 %copy-start.19 = (pred[4096]{0:T(1024)(128)(4,1)}, pred[4096]{0:T(1024)(128)(4,1)S(1)}, u32[]{:S(2)}) copy-start(pred[4096]{0:T(1024)(128)(4,1)S(1)} %get-tuple-element.163) | copy-start | bytes 12292
  249.1 5.5 collective-permute-start.1
  482.6 2.6 collective-permute-start.2
  487.8 406.9 %reduce-scatter.14.cloned.1.call-start = ((), (), s32[]{:S(2)}) async-start(), calls=%async_computation.6 | async-start | bytes 1179648
  487.9 137.1 %copy-start.11 = (f32[4,256]{1,0:T(4,128)}, f32[4,256]{1,0:T(4,128)S(1)}, u32[]{:S(2)}) copy-start(f32[4,256]{1,0:T(4,128)S(1)} %copy.300) | copy-start | bytes 12292
  619.6 5.5 collective-permute-start.3
  853.0 2.8 collective-permute-start.4
  857.8 152.6 %copy-start.14 = (pred[4096]{0:T(1024)(128)(4,1)S(1)}, pred[4096]{0:T(1024)(128)(4,1)}, u32[]{:S(2)}) copy-start(pred[4096]{0:T(1024)(128)(4,1)} %copy-done.13) | copy-start | bytes 12292
  857.8 152.6 %copy-start.16 = (pred[4096]{0:T(1024)(128)(4,1)S(1)}, pred[4096]{0:T(1024)(128)(4,1)}, u32[]{:S(2)}) copy-start(pred[4096]{0:T(1024)(128)(4,1)} %copy-done.15) | copy-start | bytes 12292
  857.8 152.6 %copy-start.18 = (pred[4096]{0:T(1024)(128)(4,1)S(1)}, pred[4096]{0:T(1024)(128)(4,1)}, u32[]{:S(2)}) copy-start(pred[4096]{0:T(1024)(128)(4,1)} %copy-done.17) | copy-start | bytes 12292
  857.9 152.6 %copy-start.20 = (pred[4096]{0:T(1024)(128)(4,1)S(1)}, pred[4096]{0:T(1024)(128)(4,1)}, u32[]{:S(2)}) copy-start(pred[4096]{0:T(1024)(128)(4,1)} %copy-done.19) | copy-start | bytes 12292
  948.3 5.5 collective-permute-start.5
  (23 other events, 788.3 us)
Sparse Core Ops, SparseCore 0:
  35.1 37.1 all-reduce.2
  201.6 36.4 reduce-scatter.9
  487.9 36.1 reduce-scatter.11
  857.9 36.7 reduce-scatter.13
where the time goes:
time: 1080 us; the launch traced here: 1070 us
  other arithmetic  437 us (40%)
  local copies, waits for them, and re-layouts  238 us (22%)
  blocking collectives  202 us (19%)
  waiting for transfers between devices  161 us (15%)
  between operations  19.6 us (2%)
    scatter-add x12, other arithmetic, knot_total(): summed.at[:, knot + tap_at].add(design * (tap_weights[tap_at] * weight_vec))  305 us
    gather x12, local copies, waits for them, and re-layouts, knot_values(): picked = jnp.take(padded, knot + tap_at, axis=1)  169 us
    unnamed x7, waiting for transfers between devices  110 us
    scatter-add x4, other arithmetic, source_total(): jnp.zeros((rows.shape[0], count), jnp.float32).at[:, source].add(rows)  90.6 us
    psum x2, blocking collectives, norm_sum(): return lax.psum(partial_value, ('sky', 'tm'))  80.7 us
    psum x3, blocking collectives, source_part(): lax.psum(source_total(obs_source, src_rows * values_obs, SRC_DEV), 'tm')  50.7 us
    gather x6, local copies, waits for them, and re-layouts, eliminate(): fitted = jnp.sum(design * jnp.take(solved, source, axis=1), axis=0)  48.9 us
    psum x1, blocking collectives, shards(): alpha_step = norm_now / lax.psum(jnp.sum(direction * mapped), ('sky', 'tm'))  39.4 us
  transfers between devices with their start and end apart: 10, of which 10 were waited for; matrix products, arithmetic and copies ran while one was open for 0% of the time, Pallas kernels for 0%

commit v1 on v0

v1 whole, which is shorter than its diff:
```python
import functools

import jax
import jax.numpy as jnp
from jax import lax
from jax.experimental import pallas as pl
from jax.experimental.pallas import tpu as pltpu
from jax.sharding import PartitionSpec as P

KN_DEV = 256
COMP = 4
TAPS = 4
PAR = 5
LANES = 128
CHUNK = 512

damping = 0.5
entry_pairs = [(row_at, col_at) for row_at in range(PAR) for col_at in range(row_at + 1)]
f32 = jnp.float32
bf16 = jnp.bfloat16


def spline_taps(phase):
    squared = phase * phase
    cubed = squared * phase
    rest = 1.0 - phase
    return (
        rest * rest * rest / 6.0,
        (3.0 * cubed - 6.0 * squared + 4.0) / 6.0,
        (-3.0 * cubed + 3.0 * squared + 3.0 * phase + 1.0) / 6.0,
        cubed / 6.0,
    )


def factorize(normal):
    factor, inverse = {}, {}
    for row_at in range(PAR):
        for col_at in range(row_at + 1):
            running = normal[row_at, col_at]
            for inner_at in range(col_at):
                running = running - factor[row_at, inner_at] * factor[col_at, inner_at]
            if row_at == col_at:
                factor[row_at, row_at] = jnp.sqrt(running)
                inverse[row_at] = 1.0 / factor[row_at, row_at]
            else:
                factor[row_at, col_at] = running * inverse[col_at]
    return factor, inverse


def chol_solve(factor, inverse, target):
    forward = []
    for row_at in range(PAR):
        running = target[row_at]
        for inner_at in range(row_at):
            running = running - factor[row_at, inner_at] * forward[inner_at]
        forward.append(running * inverse[row_at])
    result = [None] * PAR
    for row_at in reversed(range(PAR)):
        running = forward[row_at]
        for inner_at in range(row_at + 1, PAR):
            running = running - factor[inner_at, row_at] * result[inner_at]
        result[row_at] = running * inverse[row_at]
    return result


def two_parts(value):
    high = value.astype(bf16)
    low = (value - high.astype(f32)).astype(bf16)
    return jnp.concatenate([high, low], axis=0)


def joined(value):
    half = value.shape[0] // 2
    return value[:half] + value[half:]


def dot_nn(left, right):
    return lax.dot_general(left, right, (((1,), (0,)), ((), ())), preferred_element_type=f32)


def dot_nt(left, right):
    return lax.dot_general(left, right, (((1,), (1,)), ((), ())), preferred_element_type=f32)


def kernel(
    n_sky, n_tm,
    source_ref, knot_ref, count_ref, src_ref, att_ref, phase_ref, value_ref, prior_ref,
    sol_ref, res_ref, out_ref,
    hot_k, hot_s, rows_k, rows_s, y_ref, u0_ref, u1_ref,
    acc_a, acc_s, acc_k, taps_ref, z_ref,
    buf_a, buf_t, buf_c, buf_f, buf_p, buf_n,
    field_b, field_r, field_p, field_x,
    ss_t, rs_t, ss_f, rs_f, ss_p, rs_p, ss_n, rs_n,
):
    me_s = lax.axis_index("sky")
    me_t = lax.axis_index("tm")
    slots = source_ref.shape[1]
    hk = n_sky
    hs = prior_ref.shape[1] // LANES
    main = COMP * hk
    chunks = slots // CHUNK

    barrier = pltpu.get_barrier_semaphore()
    for ds in range(n_sky):
        for dt in range(n_tm):
            if ds or dt:
                pl.semaphore_signal(
                    barrier, inc=1,
                    device_id={"sky": lax.rem(me_s + ds, n_sky), "tm": lax.rem(me_t + dt, n_tm)},
                    device_id_type=pl.DeviceIdType.MESH,
                )

    def span(at):
        return pl.ds(pl.multiple_of(at * CHUNK, CHUNK), CHUNK)

    acc_a[...] = jnp.zeros_like(acc_a)

    def prepare(at, _):
        here = span(at)
        lane = lax.broadcasted_iota(jnp.int32, (1, CHUNK), 1) + at * CHUNK
        live = (lane < count_ref[0]).astype(f32)
        knot, source = knot_ref[:, here], source_ref[:, here]
        knot_low, knot_high = knot & (KN_DEV - 1), knot >> 8
        src_low, src_high = source & (LANES - 1), source >> 7
        hot_k[:, here] = (
            lax.broadcasted_iota(jnp.int32, (KN_DEV, CHUNK), 0) == knot_low
        ).astype(f32).astype(bf16)
        hot_s_here = (
            lax.broadcasted_iota(jnp.int32, (LANES, CHUNK), 0) == src_low
        ).astype(f32).astype(bf16)
        hot_s[:, here] = hot_s_here
        mask_k = (lax.broadcasted_iota(jnp.int32, (hk, CHUNK), 0) == knot_high).astype(f32)
        mask_s = (lax.broadcasted_iota(jnp.int32, (hs, CHUNK), 0) == src_high).astype(f32)
        weights = spline_taps(phase_ref[:, here])
        observed = value_ref[:, here] * live
        y_ref[:, here] = observed
        for c in range(COMP):
            design = att_ref[c : c + 1, here] * live
            for m in range(TAPS):
                base = (c * TAPS + m) * hk
                rows_k[base : base + hk, here] = mask_k * (design * weights[m])
        designs = [src_ref[e : e + 1, here] * live for e in range(PAR)]
        masked = [mask_s * design for design in designs]
        for e in range(PAR):
            rows_s[e * hs : (e + 1) * hs, here] = masked[e]
        products = jnp.concatenate(
            [masked[i] * designs[j] for i, j in entry_pairs]
            + [masked[e] * observed for e in range(PAR)],
            axis=0,
        )
        acc_a[...] += dot_nt(two_parts(products), hot_s_here)
        return 0

    lax.fori_loop(0, chunks, prepare, 0)

    def over_tm(buf, stage):
        copies = []
        for d in range(1, n_tm):
            copy = pltpu.make_async_remote_copy(
                src_ref=buf.at[me_t], dst_ref=buf.at[me_t],
                send_sem=ss_t.at[stage, d - 1], recv_sem=rs_t.at[stage, d - 1],
                device_id={"sky": me_s, "tm": lax.rem(me_t + d, n_tm)},
                device_id_type=pl.DeviceIdType.MESH,
            )
            copy.start()
            copies.append(copy)
        for copy in copies:
            copy.wait()

    def over_sky(stage):
        mine = buf_f.at[stage, me_s]
        edge = buf_f.at[stage, me_s, pl.ds(main, 8)]
        copies = []
        for ds in range(1, n_sky):
            copies.append(pltpu.make_async_remote_copy(
                src_ref=mine, dst_ref=mine,
                send_sem=ss_f.at[stage, ds - 1], recv_sem=rs_f.at[stage, ds - 1],
                device_id={"sky": lax.rem(me_s + ds, n_sky), "tm": me_t},
                device_id_type=pl.DeviceIdType.MESH,
            ))
        for ds in range(n_sky):
            copies.append(pltpu.make_async_remote_copy(
                src_ref=edge, dst_ref=buf_p.at[stage, me_s],
                send_sem=ss_p.at[stage, ds], recv_sem=rs_p.at[stage, ds],
                device_id={"sky": lax.rem(me_s + ds, n_sky), "tm": lax.rem(me_t + 1, n_tm)},
                device_id_type=pl.DeviceIdType.MESH,
            ))
            copies.append(pltpu.make_async_remote_copy(
                src_ref=edge, dst_ref=buf_n.at[stage, me_s],
                send_sem=ss_n.at[stage, ds], recv_sem=rs_n.at[stage, ds],
                device_id={"sky": lax.rem(me_s + ds, n_sky), "tm": lax.rem(me_t + n_tm - 1, n_tm)},
                device_id_type=pl.DeviceIdType.MESH,
            ))
        for copy in copies:
            copy.start()
        for copy in copies:
            copy.wait()

    def added(buf, count):
        total = buf[0]
        for at in range(1, count):
            total = total + buf[at]
        return total

    def elimination(v_of, stage):
        acc_k[...] = jnp.zeros_like(acc_k)

        def step(at, _):
            here = span(at)
            picked = joined(dot_nn(z_ref[...], hot_s[:, here]))
            fitted = jnp.sum(rows_s[:, here] * picked, axis=0, keepdims=True)
            cleaned = v_of(here) - fitted
            acc_k[...] += dot_nt(two_parts(rows_k[:, here] * cleaned), hot_k[:, here])
            return 0

        lax.fori_loop(0, chunks, step, 0)
        lane = lax.broadcasted_iota(jnp.int32, (hk, KN_DEV), 1)
        row = lax.broadcasted_iota(jnp.int32, (hk, KN_DEV), 0)
        pairs = TAPS * COMP * hk
        blocks, overs, firsts = [], [], []
        for c in range(COMP):
            block, over = None, None
            for m in range(TAPS):
                base = (c * TAPS + m) * hk
                part = acc_k[base : base + hk, :] + acc_k[pairs + base : pairs + base + hk, :]
                if m == 0:
                    block = part
                    continue
                turned = pltpu.roll(part, m, 1)
                above = pltpu.roll(turned, 1, 0)
                block = block + jnp.where(lane >= m, turned, jnp.where(row > 0, above, 0.0))
                past = jnp.where(lane[:1] < m, above[:1], 0.0)
                over = past if over is None else over + past
            blocks.append(block)
            overs.append(over)
            firsts.append(block[:1])
        buf_f[stage, me_s] = jnp.concatenate(blocks + overs + firsts, axis=0)

    def knot_field(stage):
        total = added(buf_f.at[stage], n_sky)
        before = added(buf_p.at[stage], n_sky)
        after = added(buf_n.at[stage], n_sky)
        lane = lax.broadcasted_iota(jnp.int32, (hk, KN_DEV), 1)
        row = lax.broadcasted_iota(jnp.int32, (hk, KN_DEV), 0)
        has_before = (me_t > 0).astype(f32)
        has_after = (me_t < n_tm - 1).astype(f32)
        corner = jnp.logical_and(lane < TAPS - 1, row == 0)
        blocks = []
        for c in range(COMP):
            block = total[c * hk : (c + 1) * hk]
            blocks.append(block + jnp.where(corner, before[c : c + 1] * has_before, 0.0))
        edge = (total[main : main + COMP] + after[COMP : 2 * COMP]) * has_after
        edge = jnp.where(lax.broadcasted_iota(jnp.int32, edge.shape, 1) < TAPS - 1, edge, 0.0)
        return jnp.concatenate(blocks + [edge, jnp.zeros_like(edge)], axis=0)

    def along_knots(field, u_ref):
        lane = lax.broadcasted_iota(jnp.int32, (hk, KN_DEV), 1)
        row = lax.broadcasted_iota(jnp.int32, (hk, KN_DEV), 0)
        shifts = []
        for c in range(COMP):
            block = field[c * hk : (c + 1) * hk]
            below = jnp.where(row == hk - 1, field[main + c : main + c + 1], pltpu.roll(block, hk - 1, 0))
            shifts.append(block)
            for m in range(1, TAPS):
                shifts.append(pltpu.roll(jnp.where(lane < m, below, block), KN_DEV - m, 1))
        taps_ref[...] = two_parts(jnp.concatenate(shifts, axis=0))
        acc_s[...] = jnp.zeros_like(acc_s)

        def step(at, _):
            here = span(at)
            picked = joined(dot_nn(taps_ref[...], hot_k[:, here]))
            mapped = jnp.sum(rows_k[:, here] * picked, axis=0, keepdims=True)
            u_ref[:, here] = mapped
            acc_s[...] += dot_nt(two_parts(rows_s[:, here] * mapped), hot_s[:, here])
            return 0

        lax.fori_loop(0, chunks, step, 0)
        return joined(acc_s[...])

    def tiles(value):
        return [value[e * hs : (e + 1) * hs] for e in range(PAR)]

    def scalars(*values):
        row = lax.broadcasted_iota(jnp.int32, (8, LANES), 0)
        tile = jnp.zeros((8, LANES), f32)
        for at, value in enumerate(values):
            tile = jnp.where(row == at, value, tile)
        return tile

    def inner(left, right):
        return jnp.sum(left[:main] * right[:main])

    buf_a[me_t] = joined(acc_a[...])
    pl.semaphore_wait(barrier, n_sky * n_tm - 1)
    over_tm(buf_a, 0)
    sums = added(buf_a, n_tm)
    normal = {}
    for entry_at, pair in enumerate(entry_pairs):
        entry = sums[entry_at * hs : (entry_at + 1) * hs]
        if pair[0] == pair[1]:
            e = pair[0]
            entry = entry + jnp.concatenate(
                [prior_ref[e : e + 1, h * LANES : (h + 1) * LANES] for h in range(hs)], axis=0
            )
        normal[pair] = entry
    factor, inverse = factorize(normal)
    sums_y = sums[len(entry_pairs) * hs :]

    def solved(value):
        return chol_solve(factor, inverse, tiles(value))

    def solve_into_z(value):
        z_ref[...] = two_parts(jnp.concatenate(solved(value), axis=0))

    solve_into_z(sums_y)
    elimination(lambda here: y_ref[:, here], 0)
    over_sky(0)
    field_b[...] = knot_field(0)

    size = PAR * hs
    buf_t[0, me_t, :size, :] = along_knots(field_b[...], u0_ref)
    over_tm(buf_t.at[0], 1)
    sums_0 = added(buf_t.at[0], n_tm)[:size]
    solve_into_z(sums_0)
    elimination(lambda here: u0_ref[:, here], 1)
    over_sky(1)
    b = field_b[...]
    q = knot_field(1) + damping * b
    field_x[...] = q

    buf_t[1, me_t, :size, :] = along_knots(q, u1_ref)
    buf_t[1, me_t, size:, :] = scalars(inner(b, b), inner(b, q), inner(q, q))
    over_tm(buf_t.at[1], 2)
    total = added(buf_t.at[1], n_tm)
    norm_0, b_q, q_q = (total[size + at : size + at + 1, :1] for at in range(3))
    alpha_0 = norm_0 / b_q
    norm_1 = norm_0 - alpha_0 * (2.0 * b_q - alpha_0 * q_q)
    beta_0 = norm_1 / norm_0
    sums_1 = (1.0 + beta_0) * sums_0 - alpha_0 * total[:size]
    solve_into_z(sums_1)
    residual = field_b[...] - alpha_0 * field_x[...]
    field_r[...] = residual
    field_p[...] = residual + beta_0 * field_b[...]
    elimination(lambda here: (1.0 + beta_0) * u0_ref[:, here] - alpha_0 * u1_ref[:, here], 2)
    over_sky(2)
    direction = field_p[...]
    q = knot_field(2) + damping * direction
    residual = field_r[...]
    buf_c[me_t] = scalars(inner(residual, residual), inner(direction, q))
    over_tm(buf_c, 3)
    total = added(buf_c, n_tm)
    alpha_1 = total[0:1, :1] / total[1:2, :1]
    field_x[...] = alpha_0 * field_b[...] + alpha_1 * direction
    field_r[...] = residual - alpha_1 * q
    for c in range(COMP):
        sol_ref[c] = field_x[pl.ds(c * hk + me_s, 1), :]
        res_ref[c] = field_r[pl.ds(c * hk + me_s, 1), :]
    last = solved(sums_y - alpha_0 * sums_0 - alpha_1 * sums_1)
    for e in range(PAR):
        for h in range(hs):
            out_ref[e : e + 1, h * LANES : (h + 1) * LANES] = last[e][h : h + 1]


def solution(mesh):
    n_sky, n_tm = mesh.shape["sky"], mesh.shape["tm"]

    def shards(obs_source, obs_knot, obs_count, src_design, att_design, obs_phase, obs_value, src_prior):
        slots = obs_source.shape[0]
        hk, hs = n_sky, src_prior.shape[1] // LANES
        pairs = COMP * TAPS * hk
        main = COMP * hk
        entries = len(entry_pairs) + PAR
        vmem = pl.BlockSpec(memory_space=pltpu.VMEM)
        smem = pl.BlockSpec(memory_space=pltpu.SMEM)
        dma = pltpu.SemaphoreType.DMA
        return pl.pallas_call(
            functools.partial(kernel, n_sky, n_tm),
            out_shape=(
                jax.ShapeDtypeStruct((COMP, 1, KN_DEV), f32),
                jax.ShapeDtypeStruct((COMP, 1, KN_DEV), f32),
                jax.ShapeDtypeStruct(src_prior.shape, f32),
            ),
            in_specs=[vmem, vmem, smem, vmem, vmem, vmem, vmem, vmem],
            out_specs=(vmem, vmem, vmem),
            scratch_shapes=[
                pltpu.VMEM((KN_DEV, slots), bf16),
                pltpu.VMEM((LANES, slots), bf16),
                pltpu.VMEM((pairs, slots), f32),
                pltpu.VMEM((PAR * hs, slots), f32),
                pltpu.VMEM((1, slots), f32),
                pltpu.VMEM((1, slots), f32),
                pltpu.VMEM((1, slots), f32),
                pltpu.VMEM((2 * entries * hs, LANES), f32),
                pltpu.VMEM((2 * PAR * hs, LANES), f32),
                pltpu.VMEM((2 * pairs, KN_DEV), f32),
                pltpu.VMEM((2 * pairs, KN_DEV), bf16),
                pltpu.VMEM((2 * PAR * hs, LANES), bf16),
                pltpu.VMEM((n_tm, entries * hs, LANES), f32),
                pltpu.VMEM((2, n_tm, PAR * hs + 8, LANES), f32),
                pltpu.VMEM((n_tm, 8, LANES), f32),
                pltpu.VMEM((3, n_sky, main + 8, KN_DEV), f32),
                pltpu.VMEM((3, n_sky, 8, KN_DEV), f32),
                pltpu.VMEM((3, n_sky, 8, KN_DEV), f32),
                pltpu.VMEM((main + 8, KN_DEV), f32),
                pltpu.VMEM((main + 8, KN_DEV), f32),
                pltpu.VMEM((main + 8, KN_DEV), f32),
                pltpu.VMEM((main + 8, KN_DEV), f32),
                dma((4, n_tm - 1)), dma((4, n_tm - 1)),
                dma((3, n_sky - 1)), dma((3, n_sky - 1)),
                dma((3, n_sky)), dma((3, n_sky)),
                dma((3, n_sky)), dma((3, n_sky)),
            ],
            compiler_params=pltpu.CompilerParams(collective_id=0, has_side_effects=True),
        )(
            obs_source.reshape(1, slots), obs_knot.reshape(1, slots), obs_count,
            src_design, att_design, obs_phase.reshape(1, slots), obs_value.reshape(1, slots), src_prior,
        )

    placed = (
        P(("sky", "tm")),
        P(("sky", "tm")),
        P(("sky", "tm")),
        P(None, ("sky", "tm")),
        P(None, ("sky", "tm")),
        P(("sky", "tm")),
        P(("sky", "tm")),
        P(None, "sky"),
    )
    return jax.shard_map(
        shards,
        mesh=mesh,
        in_specs=placed,
        out_specs=(P(None, "tm", "sky"), P(None, "tm", "sky"), P(None, "sky")),
        check_vma=False,
    )
```

time: 1080 us -> 70.3 us (0.07); the launches traced: 1070 us -> 70 us
  other arithmetic: 437 us -> 0 us
  local copies, waits for them, and re-layouts: 238 us -> 3.32 us
  blocking collectives: 202 us -> 0 us
  waiting for transfers between devices: 161 us -> 0 us
  Pallas kernels: 0 us -> 65.4 us
  between operations: 19.6 us -> 1.3 us
    scatter-add x16 -> x0, other arithmetic: 396 us -> none  [the longest x12 305 us: knot_total(): summed.at[:, knot + tap_at].add(design * (tap_weights[tap_at] * weight_vec))]
    gather x18 -> x0, local copies, waits for them, and re-layouts: 218 us -> none  [the longest x12 169 us: knot_values(): picked = jnp.take(padded, knot + tap_at, axis=1)]
    psum x6 -> x0, blocking collectives: 171 us -> none  [the longest x2 80.7 us: norm_sum(): return lax.psum(partial_value, ('sky', 'tm'))]
    unnamed x7 -> x0, waiting for transfers between devices: 110 us -> none
    pallas_call x0 -> x1, Pallas kernels: none -> 65.4 us  [shards(): pl.pallas_call(functools.partial(kernel, n_sky, n_tm), out_shape=(jax.Sha...]
    psum x1 -> x0, waiting for transfers between devices: 35.3 us -> none  [shards(): sums = lax.psum(source_total(obs_source, products, SRC_DEV), 'tm')]
    all_gather x3 -> x0, blocking collectives: 31 us -> none  [along_knots(): segment = lax.all_gather(field, 'sky', axis=1, tiled=True)]
    reduce_sum x9 -> x0, other arithmetic: 29.4 us -> none  [the longest x3 27.3 us: knot_values(): summed = summed + tap_weights[tap_at] * jnp.sum(design * picked, axis=0)]
  transfers between devices with their start and end apart: 10 -> 0, of which waited for: 10 -> 0; matrix products, arithmetic and copies ran while one was open for 0% -> 0% of each run, Pallas kernels for 0% -> 0%
where the time goes in v1:
time: 70.3 us; the launch traced here: 70 us
  Pallas kernels  65.4 us (93%)
  local copies, waits for them, and re-layouts  3.32 us (5%)
  between operations  1.3 us (2%)
    pallas_call x1, Pallas kernels, shards(): pl.pallas_call(functools.partial(kernel, n_sky, n_tm), out_shape=(jax.Sha...  65.4 us
    unnamed x7, local copies, waits for them, and re-layouts  3.32 us

profile of v1, /device:TPU:0, one launch (start us, length us, event | category | flops | bytes accessed | tf_op | source)
XLA Modules:
  0.0 70.0 jit_solution(16275356513775103305)
XLA Ops:
  1.3 65.4 %shard_map.103 = (f32[4,1,256]{2,1,0:T(1,128)}, f32[4,1,256]{2,1,0:T(1,128)}, f32[5,1024]{1,0:T(8,128)}) custom-call(s32[1,4096]{1,0:T(1,128)} %bitcast.4, s32[1,4096]{1,0:T(1,128)} %bitcast.5, s32[1]{0:T(128)S(6)} %copy.14.count_ref, f32[5,4096]{1,0:T(8,128)} %src_ref.1, f32[4,4096]{1,0:T(4,128)} %att_ref.1, f32[1,4096]{1,0:T(1,128)} %bitcast.6, ...), custom_call_target="tpu_custom_call" | custom-call | tf_op jit(solution)/shard_map/pallas_call | solution.py:376
  66.7 0.0 copy-start.1
  66.7 0.7 copy-done.1
  67.4 0.0 copy-start
  67.4 0.6 copy.15
  68.0 0.1 copy-done
  68.0 0.6 copy.16
  68.6 1.4 %copy.17 = f32[5,1024]{1,0:T(8,128)} copy(f32[5,1024]{1,0:T(8,128)} %get-tuple-element.8) | data formatting | bytes 40960
Async XLA Ops:
  66.7 0.7 copy-start.1
  67.4 0.7 copy-start

commit v2 on v1

--- a/solution.py
+++ b/solution.py
@@ -12,7 +12,8 @@
 TAPS = 4
 PAR = 5
 LANES = 128
-CHUNK = 512
+CHUNK = 2048
+SCALAR = 64
 
 damping = 0.5
 entry_pairs = [(row_at, col_at) for row_at in range(PAR) for col_at in range(row_at + 1)]
@@ -88,9 +89,9 @@
     sol_ref, res_ref, out_ref,
     hot_k, hot_s, rows_k, rows_s, y_ref, u0_ref, u1_ref,
     acc_a, acc_s, acc_k, taps_ref, z_ref,
-    buf_a, buf_t, buf_c, buf_f, buf_p, buf_n,
+    buf_a, buf_t, buf_f, buf_e,
     field_b, field_r, field_p, field_x,
-    ss_t, rs_t, ss_f, rs_f, ss_p, rs_p, ss_n, rs_n,
+    ss_t, rs_t, ss_f, rs_f, ss_e, rs_e,
 ):
     me_s = lax.axis_index("sky")
     me_t = lax.axis_index("tm")
@@ -119,26 +120,15 @@
         here = span(at)
         lane = lax.broadcasted_iota(jnp.int32, (1, CHUNK), 1) + at * CHUNK
         live = (lane < count_ref[0]).astype(f32)
-        knot, source = knot_ref[:, here], source_ref[:, here]
-        knot_low, knot_high = knot & (KN_DEV - 1), knot >> 8
+        source = source_ref[:, here]
         src_low, src_high = source & (LANES - 1), source >> 7
-        hot_k[:, here] = (
-            lax.broadcasted_iota(jnp.int32, (KN_DEV, CHUNK), 0) == knot_low
-        ).astype(f32).astype(bf16)
         hot_s_here = (
             lax.broadcasted_iota(jnp.int32, (LANES, CHUNK), 0) == src_low
         ).astype(f32).astype(bf16)
         hot_s[:, here] = hot_s_here
-        mask_k = (lax.broadcasted_iota(jnp.int32, (hk, CHUNK), 0) == knot_high).astype(f32)
         mask_s = (lax.broadcasted_iota(jnp.int32, (hs, CHUNK), 0) == src_high).astype(f32)
-        weights = spline_taps(phase_ref[:, here])
         observed = value_ref[:, here] * live
         y_ref[:, here] = observed
-        for c in range(COMP):
-            design = att_ref[c : c + 1, here] * live
-            for m in range(TAPS):
-                base = (c * TAPS + m) * hk
-                rows_k[base : base + hk, here] = mask_k * (design * weights[m])
         designs = [src_ref[e : e + 1, here] * live for e in range(PAR)]
         masked = [mask_s * design for design in designs]
         for e in range(PAR):
@@ -153,6 +143,24 @@
 
     lax.fori_loop(0, chunks, prepare, 0)
 
+    def prepare_knots(at, _):
+        here = span(at)
+        lane = lax.broadcasted_iota(jnp.int32, (1, CHUNK), 1) + at * CHUNK
+        live = (lane < count_ref[0]).astype(f32)
+        knot = knot_ref[:, here]
+        knot_low, knot_high = knot & (KN_DEV - 1), knot >> 8
+        hot_k[:, here] = (
+            lax.broadcasted_iota(jnp.int32, (KN_DEV, CHUNK), 0) == knot_low
+        ).astype(f32).astype(bf16)
+        mask_k = (lax.broadcasted_iota(jnp.int32, (hk, CHUNK), 0) == knot_high).astype(f32)
+        weights = spline_taps(phase_ref[:, here])
+        for c in range(COMP):
+            design = att_ref[c : c + 1, here] * live
+            for m in range(TAPS):
+                base = (c * TAPS + m) * hk
+                rows_k[base : base + hk, here] = mask_k * (design * weights[m])
+        return 0
+
     def over_tm(buf, stage):
         copies = []
         for d in range(1, n_tm):
@@ -164,12 +172,18 @@
             )
             copy.start()
             copies.append(copy)
+        return copies
+
+    def finish(copies):
         for copy in copies:
             copy.wait()
 
+    def edge_offsets(stage):
+        return range(n_tm) if stage == 2 else sorted({0, 1, n_tm - 1})
+
     def over_sky(stage):
         mine = buf_f.at[stage, me_s]
-        edge = buf_f.at[stage, me_s, pl.ds(main, 8)]
+        row = buf_e.at[stage, me_t, me_s]
         copies = []
         for ds in range(1, n_sky):
             copies.append(pltpu.make_async_remote_copy(
@@ -178,19 +192,15 @@
                 device_id={"sky": lax.rem(me_s + ds, n_sky), "tm": me_t},
                 device_id_type=pl.DeviceIdType.MESH,
             ))
-        for ds in range(n_sky):
-            copies.append(pltpu.make_async_remote_copy(
-                src_ref=edge, dst_ref=buf_p.at[stage, me_s],
-                send_sem=ss_p.at[stage, ds], recv_sem=rs_p.at[stage, ds],
-                device_id={"sky": lax.rem(me_s + ds, n_sky), "tm": lax.rem(me_t + 1, n_tm)},
-                device_id_type=pl.DeviceIdType.MESH,
-            ))
-            copies.append(pltpu.make_async_remote_copy(
-                src_ref=edge, dst_ref=buf_n.at[stage, me_s],
-                send_sem=ss_n.at[stage, ds], recv_sem=rs_n.at[stage, ds],
-                device_id={"sky": lax.rem(me_s + ds, n_sky), "tm": lax.rem(me_t + n_tm - 1, n_tm)},
-                device_id_type=pl.DeviceIdType.MESH,
-            ))
+        for dt in edge_offsets(stage):
+            for ds in range(n_sky):
+                if ds or dt:
+                    copies.append(pltpu.make_async_remote_copy(
+                        src_ref=row, dst_ref=row,
+                        send_sem=ss_e.at[stage, dt, ds], recv_sem=rs_e.at[stage, dt, ds],
+                        device_id={"sky": lax.rem(me_s + ds, n_sky), "tm": lax.rem(me_t + dt, n_tm)},
+                        device_id_type=pl.DeviceIdType.MESH,
+                    ))
         for copy in copies:
             copy.start()
         for copy in copies:
@@ -205,15 +215,16 @@
     def elimination(v_of, stage):
         acc_k[...] = jnp.zeros_like(acc_k)
 
-        def step(at, _):
+        def step(at, energy):
             here = span(at)
             picked = joined(dot_nn(z_ref[...], hot_s[:, here]))
             fitted = jnp.sum(rows_s[:, here] * picked, axis=0, keepdims=True)
-            cleaned = v_of(here) - fitted
+            value = v_of(here)
+            cleaned = value - fitted
             acc_k[...] += dot_nt(two_parts(rows_k[:, here] * cleaned), hot_k[:, here])
-            return 0
-
-        lax.fori_loop(0, chunks, step, 0)
+            return energy + value * cleaned
+
+        energy = lax.fori_loop(0, chunks, step, jnp.zeros((1, CHUNK), f32))
         lane = lax.broadcasted_iota(jnp.int32, (hk, KN_DEV), 1)
         row = lax.broadcasted_iota(jnp.int32, (hk, KN_DEV), 0)
         pairs = TAPS * COMP * hk
@@ -234,12 +245,27 @@
             blocks.append(block)
             overs.append(over)
             firsts.append(block[:1])
-        buf_f[stage, me_s] = jnp.concatenate(blocks + overs + firsts, axis=0)
+        buf_f[stage, me_s] = jnp.concatenate(blocks, axis=0)
+        edge_lane = lax.broadcasted_iota(jnp.int32, (1, LANES), 1)
+        packed = jnp.where(edge_lane == SCALAR, jnp.sum(energy, axis=1, keepdims=True), 0.0)
+        for c in range(COMP):
+            past = jnp.where(edge_lane < TAPS - 1, overs[c][:, :LANES], 0.0)
+            first = jnp.where(edge_lane < TAPS - 1, firsts[c][:, :LANES], 0.0)
+            packed = packed + (pltpu.roll(past, 8 * c, 1) if c else past) + pltpu.roll(first, 8 * (COMP + c), 1)
+        buf_e[stage, me_t, me_s] = packed
 
     def knot_field(stage):
         total = added(buf_f.at[stage], n_sky)
-        before = added(buf_p.at[stage], n_sky)
-        after = added(buf_n.at[stage], n_sky)
+        own = added(buf_e.at[stage, me_t], n_sky)
+        before = added(buf_e.at[stage, lax.rem(me_t + n_tm - 1, n_tm)], n_sky)
+        after = added(buf_e.at[stage, lax.rem(me_t + 1, n_tm)], n_sky)
+        edge_lane = lax.broadcasted_iota(jnp.int32, (1, LANES), 1)
+        rest = jnp.zeros((1, KN_DEV - LANES), f32)
+
+        def unpacked(packed, at):
+            turned = pltpu.roll(packed, LANES - 8 * at, 1) if at else packed
+            return jnp.concatenate([jnp.where(edge_lane < TAPS - 1, turned, 0.0), rest], axis=1)
+
         lane = lax.broadcasted_iota(jnp.int32, (hk, KN_DEV), 1)
         row = lax.broadcasted_iota(jnp.int32, (hk, KN_DEV), 0)
         has_before = (me_t > 0).astype(f32)
@@ -248,9 +274,10 @@
         blocks = []
         for c in range(COMP):
             block = total[c * hk : (c + 1) * hk]
-            blocks.append(block + jnp.where(corner, before[c : c + 1] * has_before, 0.0))
-        edge = (total[main : main + COMP] + after[COMP : 2 * COMP]) * has_after
-        edge = jnp.where(lax.broadcasted_iota(jnp.int32, edge.shape, 1) < TAPS - 1, edge, 0.0)
+            blocks.append(block + jnp.where(corner, unpacked(before, c) * has_before, 0.0))
+        edge = jnp.concatenate(
+            [(unpacked(own, c) + unpacked(after, COMP + c)) * has_after for c in range(COMP)], axis=0
+        )
         return jnp.concatenate(blocks + [edge, jnp.zeros_like(edge)], axis=0)
 
     def along_knots(field, u_ref):
@@ -292,7 +319,9 @@
 
     buf_a[me_t] = joined(acc_a[...])
     pl.semaphore_wait(barrier, n_sky * n_tm - 1)
-    over_tm(buf_a, 0)
+    copies = over_tm(buf_a, 0)
+    lax.fori_loop(0, chunks, prepare_knots, 0)
+    finish(copies)
     sums = added(buf_a, n_tm)
     normal = {}
     for entry_at, pair in enumerate(entry_pairs):
@@ -319,8 +348,8 @@
 
     size = PAR * hs
     buf_t[0, me_t, :size, :] = along_knots(field_b[...], u0_ref)
-    over_tm(buf_t.at[0], 1)
-    sums_0 = added(buf_t.at[0], n_tm)[:size]
+    finish(over_tm(buf_t.at[0, :, pl.ds(0, size)], 1))
+    sums_0 = added(buf_t.at[0, :, pl.ds(0, size)], n_tm)
     solve_into_z(sums_0)
     elimination(lambda here: u0_ref[:, here], 1)
     over_sky(1)
@@ -330,7 +359,7 @@
 
     buf_t[1, me_t, :size, :] = along_knots(q, u1_ref)
     buf_t[1, me_t, size:, :] = scalars(inner(b, b), inner(b, q), inner(q, q))
-    over_tm(buf_t.at[1], 2)
+    finish(over_tm(buf_t.at[1], 2))
     total = added(buf_t.at[1], n_tm)
     norm_0, b_q, q_q = (total[size + at : size + at + 1, :1] for at in range(3))
     alpha_0 = norm_0 / b_q
@@ -346,10 +375,10 @@
     direction = field_p[...]
     q = knot_field(2) + damping * direction
     residual = field_r[...]
-    buf_c[me_t] = scalars(inner(residual, residual), inner(direction, q))
-    over_tm(buf_c, 3)
-    total = added(buf_c, n_tm)
-    alpha_1 = total[0:1, :1] / total[1:2, :1]
+    energy = added(buf_e.at[2, 0], n_sky)
+    for t in range(1, n_tm):
+        energy = energy + added(buf_e.at[2, t], n_sky)
+    alpha_1 = norm_1 / (energy[:, SCALAR : SCALAR + 1] + damping * (1.0 + beta_0) * norm_1)
     field_x[...] = alpha_0 * field_b[...] + alpha_1 * direction
     field_r[...] = residual - alpha_1 * q
     for c in range(COMP):
@@ -397,18 +426,15 @@
                 pltpu.VMEM((2 * PAR * hs, LANES), bf16),
                 pltpu.VMEM((n_tm, entries * hs, LANES), f32),
                 pltpu.VMEM((2, n_tm, PAR * hs + 8, LANES), f32),
-                pltpu.VMEM((n_tm, 8, LANES), f32),
-                pltpu.VMEM((3, n_sky, main + 8, KN_DEV), f32),
-                pltpu.VMEM((3, n_sky, 8, KN_DEV), f32),
-                pltpu.VMEM((3, n_sky, 8, KN_DEV), f32),
+                pltpu.VMEM((3, n_sky, main, KN_DEV), f32),
+                pltpu.VMEM((3, n_tm, n_sky, 1, LANES), f32),
                 pltpu.VMEM((main + 8, KN_DEV), f32),
                 pltpu.VMEM((main + 8, KN_DEV), f32),
                 pltpu.VMEM((main + 8, KN_DEV), f32),
                 pltpu.VMEM((main + 8, KN_DEV), f32),
-                dma((4, n_tm - 1)), dma((4, n_tm - 1)),
+                dma((3, n_tm - 1)), dma((3, n_tm - 1)),
                 dma((3, n_sky - 1)), dma((3, n_sky - 1)),
-                dma((3, n_sky)), dma((3, n_sky)),
-                dma((3, n_sky)), dma((3, n_sky)),
+                dma((3, n_tm, n_sky)), dma((3, n_tm, n_sky)),
             ],
             compiler_params=pltpu.CompilerParams(collective_id=0, has_side_effects=True),
         )(

time: 70.3 us -> 53.8 us (0.77)
  Pallas kernels: 65.4 us -> 48.9 us
    pallas_call x1, Pallas kernels: 65.4 us -> 48.9 us  [shards(): pl.pallas_call(functools.partial(kernel, n_sky, n_tm), out_shape=(jax.Sha...]
where the time goes in v2:
time: 53.8 us; the launch traced here: 53.5 us
  Pallas kernels  48.9 us (91%)
  local copies, waits for them, and re-layouts  3.32 us (6%)
  between operations  1.3 us (2%)
    pallas_call x1, Pallas kernels, shards(): pl.pallas_call(functools.partial(kernel, n_sky, n_tm), out_shape=(jax.Sha...  48.9 us
    unnamed x7, local copies, waits for them, and re-layouts  3.32 us

profile of v2, /device:TPU:0, one launch (start us, length us, event | category | flops | bytes accessed | tf_op | source)
XLA Modules:
  0.0 53.5 jit_solution(13102513097150419447)
XLA Ops:
  1.3 48.9 %shard_map.103 = (f32[4,1,256]{2,1,0:T(1,128)}, f32[4,1,256]{2,1,0:T(1,128)}, f32[5,1024]{1,0:T(8,128)}) custom-call(s32[1,4096]{1,0:T(1,128)} %bitcast.4, s32[1,4096]{1,0:T(1,128)} %bitcast.5, s32[1]{0:T(128)S(6)} %copy.14.count_ref, f32[5,4096]{1,0:T(8,128)} %src_ref.1, f32[4,4096]{1,0:T(4,128)} %att_ref.1, f32[1,4096]{1,0:T(1,128)} %bitcast.6, ...), custom_call_target="tpu_custom_call" | custom-call | tf_op jit(solution)/shard_map/pallas_call | solution.py:405
  50.2 0.0 copy-start.1
  50.2 0.7 %copy-done.1 = f32[4,1,256]{2,1,0:T(1,128)S(1)} copy-done((f32[4,1,256]{2,1,0:T(1,128)S(1)}, f32[4,1,256]{2,1,0:T(1,128)}, u32[]{:S(2)}) %copy-start.1) | copy-done | bytes 4120
  50.9 0.0 copy-start
  50.9 0.6 %copy.15 = f32[4,1,256]{2,1,0:T(1,128)} copy(f32[4,1,256]{2,1,0:T(1,128)S(1)} %copy-done.1) | data formatting | bytes 8192
  51.4 0.1 copy-done
  51.5 0.6 %copy.16 = f32[4,1,256]{2,1,0:T(1,128)} copy(f32[4,1,256]{2,1,0:T(1,128)S(1)} %copy-done) | data formatting | bytes 8192
  52.1 1.4 %copy.17 = f32[5,1024]{1,0:T(8,128)} copy(f32[5,1024]{1,0:T(8,128)} %get-tuple-element.8) | data formatting | bytes 40960
Async XLA Ops:
  50.2 0.7 %copy-start.1 = (f32[4,1,256]{2,1,0:T(1,128)S(1)}, f32[4,1,256]{2,1,0:T(1,128)}, u32[]{:S(2)}) copy-start(f32[4,1,256]{2,1,0:T(1,128)} %get-tuple-element.6) | copy-start | bytes 12292
  50.9 0.7 %copy-start = (f32[4,1,256]{2,1,0:T(1,128)S(1)}, f32[4,1,256]{2,1,0:T(1,128)}, u32[]{:S(2)}) copy-start(f32[4,1,256]{2,1,0:T(1,128)} %get-tuple-element.7) | copy-start | bytes 12292

commit v3 on v2

--- a/solution.py
+++ b/solution.py
@@ -390,6 +390,11 @@
             out_ref[e : e + 1, h * LANES : (h + 1) * LANES] = last[e][h : h + 1]
 
 
+def hand_over(*refs):
+    for at in range(3):
+        refs[3 + at][...] = refs[at][...]
+
+
 def solution(mesh):
     n_sky, n_tm = mesh.shape["sky"], mesh.shape["tm"]
 
@@ -402,7 +407,7 @@
         vmem = pl.BlockSpec(memory_space=pltpu.VMEM)
         smem = pl.BlockSpec(memory_space=pltpu.SMEM)
         dma = pltpu.SemaphoreType.DMA
-        return pl.pallas_call(
+        results = pl.pallas_call(
             functools.partial(kernel, n_sky, n_tm),
             out_shape=(
                 jax.ShapeDtypeStruct((COMP, 1, KN_DEV), f32),
@@ -441,6 +446,12 @@
             obs_source.reshape(1, slots), obs_knot.reshape(1, slots), obs_count,
             src_design, att_design, obs_phase.reshape(1, slots), obs_value.reshape(1, slots), src_prior,
         )
+        return pl.pallas_call(
+            hand_over,
+            out_shape=tuple(jax.ShapeDtypeStruct(result.shape, f32) for result in results),
+            in_specs=[vmem] * 3,
+            out_specs=(vmem,) * 3,
+        )(*results)
 
     placed = (
         P(("sky", "tm")),

time: 53.8 us -> 51.8 us (0.963)
  local copies, waits for them, and re-layouts: 3.32 us -> 0 us
  Pallas kernels: 48.9 us -> 50.3 us
    unnamed x7 -> x0, local copies, waits for them, and re-layouts: 3.32 us -> none
    pallas_call x0 -> x1, Pallas kernels: none -> 1.4 us  [shards(): pl.pallas_call(hand_over, out_shape=tuple((jax.ShapeDtypeStruct(result.sh...]
where the time goes in v3:
time: 51.8 us; the launch traced here: 51.6 us
  Pallas kernels  50.3 us (97%)
  between operations  1.29 us (2%)
    pallas_call x1, Pallas kernels, shards(): pl.pallas_call(functools.partial(kernel, n_sky, n_tm), out_shape=(jax.Sha...  48.9 us
    pallas_call x1, Pallas kernels, shards(): pl.pallas_call(hand_over, out_shape=tuple((jax.ShapeDtypeStruct(result.sh...  1.4 us

profile of v3, /device:TPU:0, one launch (start us, length us, event | category | flops | bytes accessed | tf_op | source)
XLA Modules:
  0.0 51.6 jit_solution(1395779563807351059)
XLA Ops:
  1.3 48.9 %shard_map.103 = (f32[4,1,256]{2,1,0:T(1,128)}, f32[4,1,256]{2,1,0:T(1,128)}, f32[5,1024]{1,0:T(8,128)}) custom-call(s32[1,4096]{1,0:T(1,128)} %bitcast.4, s32[1,4096]{1,0:T(1,128)} %bitcast.5, s32[1]{0:T(128)S(6)} %copy.11.count_ref, f32[5,4096]{1,0:T(8,128)} %src_ref.1, f32[4,4096]{1,0:T(4,128)} %att_ref.1, f32[1,4096]{1,0:T(1,128)} %bitcast.6, ...), custom_call_target="tpu_custom_call" | custom-call | tf_op jit(solution)/shard_map/pallas_call | solution.py:410
  50.2 1.4 %shard_map.104 = (f32[4,1,256]{2,1,0:T(1,128)}, f32[4,1,256]{2,1,0:T(1,128)}, f32[5,1024]{1,0:T(8,128)}) custom-call(f32[4,1,256]{2,1,0:T(1,128)} %get-tuple-element.6.refs_0_, f32[4,1,256]{2,1,0:T(1,128)} %get-tuple-element.7.refs_1_, f32[5,1024]{1,0:T(8,128)} %get-tuple-element.8.refs_2_), custom_call_target="tpu_custom_call" | custom-call | tf_op jit(solution)/shard_map/pallas_call | solution.py:449
